TPU v7x, 32 devices: a whole 2x2x4 slice. The times are simulated.
32 devices in a mesh: gz: 16 (over z, y, x), gy: 2 (over core).
Axes of the slice: x: 2, y: 2, z: 4, core: 2. Of those that a mesh axis runs over, the one named last changes fastest.
Arguments:
- snapshots: float32 [48, 64, 128, 256], P(None, 'gz', 'gy'), may hold values from -6 to 6
- energies: float32 [48], replicated, may hold values from 0.3 to 3
- plane_weight: float32 [64], P('gz'), may hold values from 1 to 10
Outputs:
- modes: float32 [16, 64, 128, 256], P(None, 'gz', 'gy')
- basis: float32 [48, 16], replicated
All inputs are finite; a program needn't handle non-finite values.
Results may differ from a plain program's by a relative error of at most 0.0003.
Values sent between devices are 32-bit elements; how exact they have to be, the bound alone decides.
A program may use at most 128 MiB of HBM per device.

v0:
```python
import jax
import jax.numpy as jnp
from jax import lax
from jax.sharding import PartitionSpec as P

MODES = 16
ITERS = 6


def padded_2(block, sides, width):
    for axis, dim in sides:
        count = lax.axis_size(axis)
        forward = [(i, i + 1) for i in range(count - 1)]
        forward.append((count - 1, 0))
        backward = [(target, source) for source, target in forward]
        low = lax.ppermute(
            lax.slice_in_dim(block, block.shape[dim] - width, None, axis=dim), axis, forward
        )
        high = lax.ppermute(lax.slice_in_dim(block, 0, width, axis=dim), axis, backward)
        block = jnp.concatenate([low, block, high], axis=dim)
    return block


def local(snapshots, energies, plane_weight):
    count, planes, rows, width = snapshots.shape
    total = planes * lax.axis_size("gz") * rows * lax.axis_size("gy") * width
    scaled = snapshots * energies[:, None, None, None]
    padded = padded_2(scaled, (("gz", 1),), 1)
    filtered = 0.25 * padded[:, :-2] + 0.5 * scaled + 0.25 * padded[:, 2:]
    flat = filtered.reshape(count, -1)
    weighted = (filtered * plane_weight[None, :, None, None]).reshape(count, -1)
    partial_value = jnp.dot(weighted, flat.T, precision=lax.Precision.HIGHEST) / total
    gram = lax.psum(partial_value, ("gz", "gy"))
    basis = jnp.eye(count, dtype=jnp.float32)[:, :MODES]
    for step in range(ITERS):
        image = jnp.dot(gram, basis, precision=lax.Precision.HIGHEST)
        factor = jnp.linalg.cholesky(jnp.dot(image.T, image, precision=lax.Precision.HIGHEST))
        basis = jax.scipy.linalg.solve_triangular(factor, image.T, lower=True).T
    raw = jnp.dot(basis.T, flat, precision=lax.Precision.HIGHEST).reshape(
        MODES, planes, rows, width
    )
    projected = jnp.dot(gram, basis, precision=lax.Precision.HIGHEST)
    norms = jnp.sum(basis * projected, axis=0)
    modes = raw / jnp.sqrt(norms)[:, None, None, None]
    return (modes, basis)


def solution(mesh):
    placed = (P(None, "gz", "gy", None), P(), P("gz"))
    return jax.shard_map(
        local,
        mesh=mesh,
        in_specs=placed,
        out_specs=(P(None, "gz", "gy", None), P()),
        check_vma=False,
    )
```

profile of v0, /device:TPU:0, one launch (start us, length us, event | category | flops | bytes accessed | tf_op | source)
XLA Modules:
  0.0 292.3 jit_solution(18266743144551200550)
XLA Ops:
  0.6 12.0 %broadcast_multiply_fusion.1 = f32[48,4,64,256]{3,2,1,0:T(8,128)} fusion(f32[48,4,64,256]{3,2,1,0:T(8,128)} %param.6, f32[48]{0:T(128)} %param.7), kind=kLoop, calls=%fused_computation.12 | loop fusion | flops 3145728 | bytes 25166016 | tf_op jit(solution)/shard_map/mul | solution.py:27
  12.7 0.0 copy-start
  12.7 3.7 %fusion.67 = (f32[48,1,64,256]{3,2,1,0:T(8,128)S(1)}, f32[48,1,64,256]{3,2,1,0:T(8,128)S(1)}) fusion(f32[48,4,64,256]{3,2,1,0:T(8,128)} %broadcast_multiply_fusion.1), kind=kLoop, calls=%fused_computation.84 | loop fusion | bytes 12582912 | tf_op jit(solution)/shard_map/slice | solution.py:17
  16.4 3.0 %collective-permute-start = (f32[48,1,64,256]{3,2,1,0:T(8,128)S(1)}, f32[48,1,64,256]{3,2,1,0:T(8,128)}, u32[]{:S(2)}, u32[]{:S(2)}) collective-permute-start(f32[48,1,64,256]{3,2,1,0:T(8,128)S(1)} %get-tuple-element.10), channel_id=1, source_target_pairs={{0,2},{2,4},{4,6},{6,8},{8,10},{10,12},{12,14},{14,16},{16,18},{18... | collective-permute-start | bytes 9437192 | tf_op jit(solution)/shard_map/ppermute | solution.py:16
  19.4 4.1 %collective-permute-start.1 = (f32[48,1,64,256]{3,2,1,0:T(8,128)S(1)}, f32[48,1,64,256]{3,2,1,0:T(8,128)}, u32[]{:S(2)}, u32[]{:S(2)}) collective-permute-start(f32[48,1,64,256]{3,2,1,0:T(8,128)S(1)} %get-tuple-element.11), channel_id=1, source_target_pairs={{2,0},{4,2},{6,4},{8,6},{10,8},{12,10},{14,12},{16,14},{18,16},{20... | collective-permute-start | bytes 9437192 | tf_op jit(solution)/shard_map/ppermute | solution.py:19
  23.5 130.7 %collective-permute-done = f32[48,1,64,256]{3,2,1,0:T(8,128)} collective-permute-done((f32[48,1,64,256]{3,2,1,0:T(8,128)S(1)}, f32[48,1,64,256]{3,2,1,0:T(8,128)}, u32[]{:S(2)}, u32[]{:S(2)}) %collective-permute-start) | collective-permute-done | bytes 3145760 | tf_op jit(solution)/shard_map/ppermute | solution.py:16
  154.2 2.1 collective-permute-done.1
  156.2 0.0 copy-done
  156.2 0.0 copy-done.2
  156.3 13.5 %broadcast_multiply_fusion = (f32[48,4,64,256]{3,2,1,0:T(8,128)}, f32[48,4,64,256]{3,2,1,0:T(8,128)}) fusion(f32[4]{0:T(128)S(1)} %copy-done.2, f32[48,1,64,256]{3,2,1,0:T(8,128)} %collective-permute-done.1, f32[48,4,64,256]{3,2,1,0:T(8,128)S(1)} %copy-done, f32[48,1,64,256]{3,2,1,0:T(8,128)} %collective-permute-done), kind=kLoop, calls=%fused_computation.11 | loop fusion | flops 25165824 | bytes 44040208 | tf_op jit(solution)/shard_map/mul | solution.py:31
  169.7 32.1 %fusion.16 = f32[48,48]{1,0:T(8,128)S(1)} fusion(f32[48,4,64,256]{3,2,1,0:T(8,128)} %get-tuple-element.9, f32[48,4,64,256]{3,2,1,0:T(8,128)} %get-tuple-element.8), kind=kOutput, calls=%fused_computation.15 | convolution fusion | flops 1811941632 | bytes 25175040 | tf_op jit(solution)/shard_map/dot_general | solution.py:32
  201.8 39.7 %psum.7 = f32[48,48]{1,0:T(8,128)S(1)} all-reduce(f32[48,48]{1,0:T(8,128)S(1)} %fusion.16), channel_id=1, replica_groups=mesh['gz'=16,'gy'=2] {'gz','gy'}, use_global_device_ids=true, to_apply=%region_0.0 | all-reduce | flops 2304 | bytes 18432 | tf_op jit(solution)/shard_map/psum | solution.py:33
  241.6 0.2 fusion.22
  241.8 0.1 fusion.68
  241.9 0.1 copy.16
  242.0 1.5 cholesky.104
  243.5 0.6 compare_reduce_fusion.5
  244.1 0.6 fusion.24
  244.8 1.2 custom-call.10
  246.0 0.2 fusion.51
  246.2 0.2 fusion.69
  246.4 0.1 fusion.70
  246.5 0.1 copy.17
  246.6 1.5 cholesky.115
  248.1 0.6 compare_reduce_fusion.4
  248.8 0.6 fusion.25
  249.4 1.2 custom-call.11
  250.6 0.2 fusion.47
  250.8 0.2 fusion.71
  251.0 0.1 fusion.72
  251.1 0.1 copy.18
  251.2 1.5 cholesky.126
  252.7 0.6 compare_reduce_fusion.3
  253.4 0.6 fusion.26
  254.0 1.2 custom-call.12
  255.3 0.2 fusion.43
  255.5 0.2 fusion.73
  255.6 0.1 fusion.74
  255.8 0.1 copy.19
  255.8 1.5 cholesky.137
  257.4 0.6 compare_reduce_fusion.2
  258.0 0.6 fusion.27
  258.7 1.2 custom-call.13
  259.9 0.2 fusion.39
  260.1 0.2 fusion.75
  260.2 0.1 fusion.76
  260.4 0.1 copy.20
  260.5 1.5 cholesky.148
  262.0 0.6 compare_reduce_fusion.1
  262.6 0.6 fusion.28
  263.3 1.2 custom-call.14
  264.5 0.2 fusion.35
  264.7 0.2 fusion.77
  264.9 0.1 fusion.78
  265.0 0.1 copy.21
  265.1 1.5 cholesky.159
  266.6 0.6 compare_reduce_fusion
  267.2 0.6 fusion.29
  267.9 1.2 custom-call.15
  269.1 0.2 fusion.31
  269.3 0.3 fusion.21
  269.6 18.2 %broadcast_divide_fusion = f32[16,4,64,256]{3,0,2,1:T(8,128)S(1)} fusion(f32[16]{0:T(128)S(1)} %sqrt.7, f32[4,64,256,48]{2,1,0,3:T(8,128)} %bitcast.120, f32[16,48]{1,0:T(8,128)S(1)} %fusion.31), kind=kOutput, calls=%fused_computation.13 | convolution fusion | flops 605028352 | bytes 16780352 | tf_op jit(solution)/shard_map/dot_general | solution.py:39
  287.8 4.4 %copy.23 = f32[16,4,64,256]{3,2,1,0:T(8,128)} copy(f32[16,4,64,256]{3,0,2,1:T(8,128)S(1)} %broadcast_divide_fusion) | data formatting | bytes 8388608
  292.3 0.0 copy-done.1
  (15 shorter events, 0.2 us)
Async XLA Ops:
  12.7 143.6 %copy-start = (f32[48,4,64,256]{3,2,1,0:T(8,128)S(1)}, f32[48,4,64,256]{3,2,1,0:T(8,128)}, u32[]{:S(2)}) copy-start(f32[48,4,64,256]{3,2,1,0:T(8,128)} %broadcast_multiply_fusion.1) | copy-start | bytes 37748740
  12.7 143.6 %copy-start.2 = (f32[4]{0:T(128)S(1)}, f32[4]{0:T(128)}, u32[]{:S(2)}) copy-start(f32[4]{0:T(128)} %param.8) | copy-start | bytes 52
  16.4 137.8 %collective-permute-start = (f32[48,1,64,256]{3,2,1,0:T(8,128)S(1)}, f32[48,1,64,256]{3,2,1,0:T(8,128)}, u32[]{:S(2)}, u32[]{:S(2)}) collective-permute-start(f32[48,1,64,256]{3,2,1,0:T(8,128)S(1)} %get-tuple-element.10), channel_id=1, source_target_pairs={{0,2},{2,4},{4,6},{6,8},{8,10},{10,12},{12,14},{14,16},{16,18},{18... | collective-permute-start | bytes 9437192 | tf_op jit(solution)/shard_map/ppermute | solution.py:16
  19.4 136.8 %collective-permute-start.1 = (f32[48,1,64,256]{3,2,1,0:T(8,128)S(1)}, f32[48,1,64,256]{3,2,1,0:T(8,128)}, u32[]{:S(2)}, u32[]{:S(2)}) collective-permute-start(f32[48,1,64,256]{3,2,1,0:T(8,128)S(1)} %get-tuple-element.11), channel_id=1, source_target_pairs={{2,0},{4,2},{6,4},{8,6},{10,8},{12,10},{14,12},{16,14},{18,16},{20... | collective-permute-start | bytes 9437192 | tf_op jit(solution)/shard_map/ppermute | solution.py:19
  269.3 22.9 %copy-start.1 = (f32[16,48]{1,0:T(8,128)}, f32[16,48]{1,0:T(8,128)S(1)}, u32[]{:S(2)}) copy-start(f32[16,48]{1,0:T(8,128)S(1)} %fusion.31) | copy-start | bytes 9220
where the time goes:
time: 293 us; the launch traced here: 292 us
  waiting for transfers between devices  133 us (45%)
  matrix products  53.6 us (18%)
  other arithmetic  49.7 us (17%)
  blocking collectives  39.7 us (14%)
  local copies, waits for them, and re-layouts  8.63 us (3%)
  starting transfers between devices  7.08 us (2%)
    ppermute x1, waiting for transfers between devices, padded_2(): lax.ppermute(lax.slice_in_dim(block, block.shape[dim] - width, None, axis...  131 us
    psum x1, blocking collectives, local(): gram = lax.psum(partial_value, ('gz', 'gy'))  39.7 us
    dot_general x1, matrix products, local(): jnp.dot(weighted, flat.T, precision=lax.Precision.HIGHEST) / total  32.1 us
    dot_general x1, matrix products, local(): jnp.dot(basis.T, flat, precision=lax.Precision.HIGHEST)  18.2 us
    mul x1, other arithmetic, local(): weighted = (filtered * plane_weight[None, :, None, None]).reshape(count, -1)  13.5 us
    another operation x18, other arithmetic, local(): jnp.linalg.cholesky(jnp.dot(image.T, image, precision=lax.Precision.HIGHE...  12.9 us
    mul x1, other arithmetic, local(): scaled = snapshots * energies[:, None, None, None]  12 us
    another operation x12, other arithmetic, local(): basis = jax.scipy.linalg.solve_triangular(factor, image.T, lower=True).T  11.3 us
  transfers between devices with their start and end apart: 2, of which 2 were waited for; matrix products, arithmetic and copies ran while one was open for 0% of the time, Pallas kernels for 0%

commit v1 on v0

--- a/solution.py
+++ b/solution.py
@@ -30,7 +30,10 @@
     flat = filtered.reshape(count, -1)
     weighted = (filtered * plane_weight[None, :, None, None]).reshape(count, -1)
     partial_value = jnp.dot(weighted, flat.T, precision=lax.Precision.HIGHEST) / total
-    gram = lax.psum(partial_value, ("gz", "gy"))
+    fields_launch = lambda piece_in, axis_key, lane_axis: lax.psum(
+        lax.psum(piece_in, axis_key), lane_axis
+    )
+    gram = fields_launch(partial_value, "gy", "gz")
     basis = jnp.eye(count, dtype=jnp.float32)[:, :MODES]
     for step in range(ITERS):
         image = jnp.dot(gram, basis, precision=lax.Precision.HIGHEST)

time: 293 us -> 331 us (1.13)
  blocking collectives: 39.7 us -> 78.3 us
    psum x1 -> x2, blocking collectives: 39.7 us -> 78.3 us  [the longest x1 74.9 us: local(): lax.psum(lax.psum(piece_in, axis_key), lane_axis)]
where the time goes in v1:
time: 331 us
  waiting for transfers between devices  133 us (40%)
  blocking collectives  78.3 us (24%)
  matrix products  53.6 us (16%)
  other arithmetic  49.7 us (15%)
  local copies, waits for them, and re-layouts  8.63 us (3%)
  starting transfers between devices  7.08 us (2%)
    ppermute x1, waiting for transfers between devices, padded_2(): lax.ppermute(lax.slice_in_dim(block, block.shape[dim] - width, None, axis...  131 us
    psum x1, blocking collectives, local(): lax.psum(lax.psum(piece_in, axis_key), lane_axis)  74.9 us
    dot_general x1, matrix products, local(): jnp.dot(weighted, flat.T, precision=lax.Precision.HIGHEST) / total  32.1 us
    dot_general x1, matrix products, local(): jnp.dot(basis.T, flat, precision=lax.Precision.HIGHEST)  18.2 us
    mul x1, other arithmetic, local(): weighted = (filtered * plane_weight[None, :, None, None]).reshape(count, -1)  13.5 us
    another operation x18, other arithmetic, local(): jnp.linalg.cholesky(jnp.dot(image.T, image, precision=lax.Precision.HIGHE...  12.9 us
    mul x1, other arithmetic, local(): scaled = snapshots * energies[:, None, None, None]  12 us
    another operation x12, other arithmetic, local(): basis = jax.scipy.linalg.solve_triangular(factor, image.T, lower=True).T  11.3 us
  transfers between devices with their start and end apart: 2, of which 2 were waited for; matrix products, arithmetic and copies ran while one was open for 0% of the time, Pallas kernels for 0%

profile of v1, /device:TPU:0, one launch (start us, length us, event | category | flops | bytes accessed | tf_op | source)
XLA Modules:
  0.0 330.9 jit_solution(10026306394363154525)
XLA Ops:
  0.6 12.0 %broadcast_multiply_fusion.1 = f32[48,4,64,256]{3,2,1,0:T(8,128)} fusion(f32[48,4,64,256]{3,2,1,0:T(8,128)} %param.6, f32[48]{0:T(128)} %param.7), kind=kLoop, calls=%fused_computation.12 | loop fusion | flops 3145728 | bytes 25166016 | tf_op jit(solution)/shard_map/mul | solution.py:27
  12.7 3.7 %fusion.67 = (f32[48,1,64,256]{3,2,1,0:T(8,128)S(1)}, f32[48,1,64,256]{3,2,1,0:T(8,128)S(1)}) fusion(f32[48,4,64,256]{3,2,1,0:T(8,128)} %broadcast_multiply_fusion.1), kind=kLoop, calls=%fused_computation.84 | loop fusion | bytes 12582912 | tf_op jit(solution)/shard_map/slice | solution.py:17
  16.4 3.0 collective-permute-start
  19.4 4.1 %collective-permute-start.1 = (f32[48,1,64,256]{3,2,1,0:T(8,128)S(1)}, f32[48,1,64,256]{3,2,1,0:T(8,128)}, u32[]{:S(2)}, u32[]{:S(2)}) collective-permute-start(f32[48,1,64,256]{3,2,1,0:T(8,128)S(1)} %get-tuple-element.11), channel_id=1, source_target_pairs={{2,0},{4,2},{6,4},{8,6},{10,8},{12,10},{14,12},{16,14},{18,16},{20... | collective-permute-start | bytes 9437192 | tf_op jit(solution)/shard_map/ppermute | solution.py:19
  23.5 130.7 %collective-permute-done = f32[48,1,64,256]{3,2,1,0:T(8,128)} collective-permute-done((f32[48,1,64,256]{3,2,1,0:T(8,128)S(1)}, f32[48,1,64,256]{3,2,1,0:T(8,128)}, u32[]{:S(2)}, u32[]{:S(2)}) %collective-permute-start) | collective-permute-done | bytes 3145760 | tf_op jit(solution)/shard_map/ppermute | solution.py:16
  154.2 2.1 collective-permute-done.1
  156.2 0.0 copy-done
  156.2 0.0 copy-done.2
  156.3 13.5 %broadcast_multiply_fusion = (f32[48,4,64,256]{3,2,1,0:T(8,128)}, f32[48,4,64,256]{3,2,1,0:T(8,128)}) fusion(f32[4]{0:T(128)S(1)} %copy-done.2, f32[48,1,64,256]{3,2,1,0:T(8,128)} %collective-permute-done.1, f32[48,4,64,256]{3,2,1,0:T(8,128)S(1)} %copy-done, f32[48,1,64,256]{3,2,1,0:T(8,128)} %collective-permute-done), kind=kLoop, calls=%fused_computation.11 | loop fusion | flops 25165824 | bytes 44040208 | tf_op jit(solution)/shard_map/mul | solution.py:31
  169.7 32.1 %fusion.16 = f32[48,48]{1,0:T(8,128)S(1)} fusion(f32[48,4,64,256]{3,2,1,0:T(8,128)} %get-tuple-element.9, f32[48,4,64,256]{3,2,1,0:T(8,128)} %get-tuple-element.8), kind=kOutput, calls=%fused_computation.15 | convolution fusion | flops 1811941632 | bytes 25175040 | tf_op jit(solution)/shard_map/dot_general | solution.py:32
  201.8 3.4 %psum.14 = f32[48,48]{1,0:T(8,128)S(1)} all-reduce(f32[48,48]{1,0:T(8,128)S(1)} %fusion.16), channel_id=1, replica_groups=mesh['gz'=16,'gy'=2] {'gy'}, use_global_device_ids=true, to_apply=%region_0.0 | all-reduce | flops 2304 | bytes 18432 | tf_op jit(solution)/shard_map/psum | solution.py:34
  205.3 74.9 %psum.15 = f32[48,48]{1,0:T(8,128)S(1)} all-reduce(f32[48,48]{1,0:T(8,128)S(1)} %psum.14), channel_id=1, replica_groups=mesh['gz'=16,'gy'=2] {'gz'}, use_global_device_ids=true, to_apply=%region_1.0 | all-reduce | flops 2304 | bytes 18432 | tf_op jit(solution)/shard_map/psum | solution.py:33
  280.2 0.2 fusion.22
  280.4 0.1 fusion.68
  280.5 0.1 copy.16
  280.6 1.5 cholesky.104
  282.1 0.6 compare_reduce_fusion.5
  282.7 0.6 fusion.24
  283.4 1.2 custom-call.10
  284.6 0.2 fusion.51
  284.8 0.2 fusion.69
  285.0 0.1 fusion.70
  285.1 0.1 copy.17
  285.2 1.5 cholesky.115
  286.7 0.6 compare_reduce_fusion.4
  287.4 0.6 fusion.25
  288.0 1.2 custom-call.11
  289.2 0.2 fusion.47
  289.4 0.2 fusion.71
  289.6 0.1 fusion.72
  289.8 0.1 copy.18
  289.8 1.5 cholesky.126
  291.3 0.6 compare_reduce_fusion.3
  292.0 0.6 fusion.26
  292.6 1.2 custom-call.12
  293.9 0.2 fusion.43
  294.1 0.2 fusion.73
  294.2 0.1 fusion.74
  294.4 0.1 copy.19
  294.5 1.5 cholesky.137
  296.0 0.6 compare_reduce_fusion.2
  296.6 0.6 fusion.27
  297.3 1.2 custom-call.13
  298.5 0.2 fusion.39
  298.7 0.2 fusion.75
  298.8 0.1 fusion.76
  299.0 0.1 copy.20
  299.1 1.5 cholesky.148
  300.6 0.6 compare_reduce_fusion.1
  301.2 0.6 fusion.28
  301.9 1.2 custom-call.14
  303.1 0.2 fusion.35
  303.3 0.2 fusion.77
  303.5 0.1 fusion.78
  303.6 0.1 copy.21
  303.7 1.5 cholesky.159
  305.2 0.6 compare_reduce_fusion
  305.9 0.6 fusion.29
  306.5 1.2 custom-call.15
  307.7 0.2 fusion.31
  307.9 0.3 fusion.21
  308.2 18.2 %broadcast_divide_fusion = f32[16,4,64,256]{3,0,2,1:T(8,128)S(1)} fusion(f32[16]{0:T(128)S(1)} %sqrt.7, f32[4,64,256,48]{2,1,0,3:T(8,128)} %bitcast.120, f32[16,48]{1,0:T(8,128)S(1)} %fusion.31), kind=kOutput, calls=%fused_computation.13 | convolution fusion | flops 605028352 | bytes 16780352 | tf_op jit(solution)/shard_map/dot_general | solution.py:42
  326.4 4.4 %copy.23 = f32[16,4,64,256]{3,2,1,0:T(8,128)} copy(f32[16,4,64,256]{3,0,2,1:T(8,128)S(1)} %broadcast_divide_fusion) | data formatting | bytes 8388608
  330.9 0.0 copy-done.1
  (16 shorter events, 0.2 us)
Async XLA Ops:
  12.7 143.6 %copy-start = (f32[48,4,64,256]{3,2,1,0:T(8,128)S(1)}, f32[48,4,64,256]{3,2,1,0:T(8,128)}, u32[]{:S(2)}) copy-start(f32[48,4,64,256]{3,2,1,0:T(8,128)} %broadcast_multiply_fusion.1) | copy-start | bytes 37748740
  12.7 143.6 %copy-start.2 = (f32[4]{0:T(128)S(1)}, f32[4]{0:T(128)}, u32[]{:S(2)}) copy-start(f32[4]{0:T(128)} %param.8) | copy-start | bytes 52
  16.4 137.8 %collective-permute-start = (f32[48,1,64,256]{3,2,1,0:T(8,128)S(1)}, f32[48,1,64,256]{3,2,1,0:T(8,128)}, u32[]{:S(2)}, u32[]{:S(2)}) collective-permute-start(f32[48,1,64,256]{3,2,1,0:T(8,128)S(1)} %get-tuple-element.10), channel_id=1, source_target_pairs={{0,2},{2,4},{4,6},{6,8},{8,10},{10,12},{12,14},{14,16},{16,18},{18... | collective-permute-start | bytes 9437192 | tf_op jit(solution)/shard_map/ppermute | solution.py:16
  19.4 136.8 %collective-permute-start.1 = (f32[48,1,64,256]{3,2,1,0:T(8,128)S(1)}, f32[48,1,64,256]{3,2,1,0:T(8,128)}, u32[]{:S(2)}, u32[]{:S(2)}) collective-permute-start(f32[48,1,64,256]{3,2,1,0:T(8,128)S(1)} %get-tuple-element.11), channel_id=1, source_target_pairs={{2,0},{4,2},{6,4},{8,6},{10,8},{12,10},{14,12},{16,14},{18,16},{20... | collective-permute-start | bytes 9437192 | tf_op jit(solution)/shard_map/ppermute | solution.py:19
  307.9 22.9 %copy-start.1 = (f32[16,48]{1,0:T(8,128)}, f32[16,48]{1,0:T(8,128)S(1)}, u32[]{:S(2)}) copy-start(f32[16,48]{1,0:T(8,128)S(1)} %fusion.31) | copy-start | bytes 9220
